TPU v7x, 32 devices: a whole 2x2x4 slice. The times are simulated.
32 devices in a mesh: cfg: 2 (over y), space: 8 (over z, x), tm: 2 (over core).
Axes of the slice: x: 2, y: 2, z: 4, core: 2. Of those that a mesh axis runs over, the one named last changes fastest.
Arguments:
- eigvecs: bfloat16 [4, 2304, 3, 2, 128], P(('cfg', 'tm'), 'space'), parts along dimension 0, may hold values from -6 to 6
- perambulator: bfloat16 [4, 8, 4, 2, 128, 128], P(('cfg', 'tm'), None, None, None, 'space'), parts along dimension 0, may hold values from -1 to 4
- momenta: int32 [1, 3], replicated, may hold values from 1 to 3
- source_slots: int32 [2], replicated, may hold values from 0 to 7, as said below
- gamma_columns: int32 [12, 4], replicated, may hold values from 0 to 3, each once within a row
- gamma_phases: int32 [12, 4], replicated, may hold values from 0 to 3
Outputs:
- meson: float32 [4, 128, 1, 12, 2, 128], P(('cfg', 'tm'), 'space'), parts along dimension 0
There are 2 independent parts, one for each index of `cfg`. A program takes and returns all parts, laid end to end along the dimension named above; an argument that names none is the same for every part. Nothing has to cross between parts.
Inputs may be any that keep to these rules, and one draw needn't show every extreme that they name: `source_slots`: the two slots differ, and one of them is 7. `gamma_columns`: each row is a permutation of 0 to 3.
All inputs are finite; a program needn't handle non-finite values.
Results may differ from a plain program's by a relative error of at most 0.0049.
Values may be sent and summed in bfloat16 or wider, within the bound.
No kernel may reach another device: no remote copies, remote signals or barrier semaphores. Data moves between devices by JAX's collectives and lax.ppermute only.
A program may use at most 64 MiB of HBM per device.

v0:
```python
import math
import jax
import jax.numpy as jnp
from jax import lax
from jax.sharding import PartitionSpec as P

LY = 48
LZ = 48


def gamma_mixer(gamma_columns, gamma_phases):
    spin_ids = jnp.arange(4, dtype=jnp.int32)
    matches = (gamma_columns[:, :, None] == spin_ids[None, None, :]).astype(jnp.float32)
    real_sign = (gamma_phases == 0).astype(jnp.float32) - (gamma_phases == 2).astype(jnp.float32)
    imag_sign = (gamma_phases == 1).astype(jnp.float32) - (gamma_phases == 3).astype(jnp.float32)
    real_part = matches * real_sign[:, :, None]
    imag_part = matches * imag_sign[:, :, None]
    first_row = jnp.stack([real_part, -imag_part], axis=-1)
    second_row = jnp.stack([imag_part, real_part], axis=-1)
    return jnp.stack([first_row, second_row], axis=1)


def apply_gammas(blocks, gamma_mix, factor):
    return factor * jnp.einsum(
        "gostk,apstkb->apgob", gamma_mix, blocks, precision=lax.Precision.HIGHEST
    )


def phase_tables(momenta, site_ids, extent_x):
    coord_z = site_ids % LZ
    coord_y = site_ids // LZ % LY
    coord_x = site_ids // (LY * LZ)
    turns = (
        (momenta[:, 0:1] * coord_x[None, :] % extent_x).astype(jnp.float32) / extent_x
        + (momenta[:, 1:2] * coord_y[None, :] % LY).astype(jnp.float32) / LY
        + (momenta[:, 2:3] * coord_z[None, :] % LZ).astype(jnp.float32) / LZ
    )
    angles = 2.0 * math.pi * turns
    return (jnp.cos(angles), jnp.sin(angles))


def sink_vectors(vectors, picked):
    eig_count = picked.shape[-1]
    real_parts = []
    imag_parts = []
    for spin_index in range(4):
        real_tau = picked[spin_index, 0]
        imag_tau = picked[spin_index, 1]
        stacked = jnp.concatenate(
            [
                jnp.concatenate([real_tau, imag_tau], axis=1),
                jnp.concatenate([-imag_tau, real_tau], axis=1),
            ],
            axis=0,
        )
        product = jnp.dot(vectors, stacked, preferred_element_type=jnp.float32).astype(jnp.bfloat16)
        real_parts.append(product[:, :eig_count])
        imag_parts.append(product[:, eig_count:])
    return (jnp.stack(real_parts, axis=1), jnp.stack(imag_parts, axis=1))


def twisted(right_real, right_imag, cosine, sine):
    moment_count, site_count = cosine.shape
    shaped_real = right_real.astype(jnp.float32).reshape(1, site_count, 3, 4, -1)
    shaped_imag = right_imag.astype(jnp.float32).reshape(1, site_count, 3, 4, -1)
    cosine_wide = cosine.reshape(moment_count, site_count, 1, 1, 1)
    sine_wide = sine.reshape(moment_count, site_count, 1, 1, 1)
    wave_real = (cosine_wide * shaped_real - sine_wide * shaped_imag).astype(jnp.bfloat16)
    wave_imag = (sine_wide * shaped_real + cosine_wide * shaped_imag).astype(jnp.bfloat16)
    return (
        wave_real.reshape(moment_count, site_count * 3, 4, -1),
        wave_imag.reshape(moment_count, site_count * 3, 4, -1),
    )


def on_device(eigvecs, perambulator, momenta, source_slots, gamma_columns, gamma_phases):
    local_sites = eigvecs.shape[1]
    eig_count = eigvecs.shape[4]
    ranks = lax.axis_size("space")
    total_sites = local_sites * ranks
    extent_x = total_sites // (LY * LZ)
    factor = 1.0 / math.sqrt(12.0 * total_sites)
    site_ids = lax.axis_index("space") * local_sites + jnp.arange(local_sites, dtype=jnp.int32)
    cosine, sine = phase_tables(momenta, site_ids, extent_x)
    gamma_mix = gamma_mixer(gamma_columns, gamma_phases)
    gathered = lax.all_gather(perambulator, "space", axis=4, tiled=True)
    chosen = jnp.take(gathered, source_slots, axis=1)
    vectors = eigvecs[0].reshape(local_sites * 3, 2 * eig_count)
    left_real, left_imag = sink_vectors(vectors, chosen[0, 0])
    right_real, right_imag = sink_vectors(vectors, chosen[0, 1])
    wave_real, wave_imag = twisted(right_real, right_imag, cosine, sine)
    real_block = jnp.einsum(
        "rsa,rtb->astb", left_real, wave_real[0], preferred_element_type=jnp.float32
    ) + jnp.einsum("rsa,rtb->astb", left_imag, wave_imag[0], preferred_element_type=jnp.float32)
    imag_block = jnp.einsum(
        "rsa,rtb->astb", left_real, wave_imag[0], preferred_element_type=jnp.float32
    ) - jnp.einsum("rsa,rtb->astb", left_imag, wave_real[0], preferred_element_type=jnp.float32)
    per_momentum = [jnp.stack([real_block, imag_block], axis=3)]
    meson_rows = lax.psum_scatter(
        apply_gammas(jnp.stack(per_momentum, axis=1), gamma_mix, factor),
        "space",
        scatter_dimension=0,
        tiled=True,
    )
    results = [meson_rows]
    return jnp.stack(results, axis=0)


def solution(mesh):
    in_specs = (
        P(("cfg", "tm"), "space", None, None, None),
        P(("cfg", "tm"), None, None, None, "space", None),
        P(),
        P(),
        P(),
        P(),
    )
    out_specs = P(("cfg", "tm"), "space", None, None, None, None)
    return jax.shard_map(
        on_device, mesh=mesh, in_specs=in_specs, out_specs=out_specs, check_vma=False
    )
```

profile of v0, /device:TPU:0, one launch (start us, length us, event | category | flops | bytes accessed | tf_op | source)
XLA Modules:
  0.0 155.9 jit_solution(15535519684010389070)
XLA Ops:
  6.5 0.0 all-gather.2.cloned.1.call-start
  6.5 0.7 all-gather.2.cloned.1.call-update
  7.3 0.0 reduce-scatter.2.cloned.1.call-start
  7.3 1.3 fusion.137
  8.6 1.3 fusion.109
  9.9 0.1 mul.153
  10.0 0.2 mul.154
  10.2 0.1 mul.157
  10.3 0.2 mul.158
  10.5 0.7 compare_select_fusion
  11.2 0.7 convert_subtract_fusion
  11.9 0.7 fusion.124
  12.6 0.7 compare_and_fusion
  13.3 49.2 %all-gather.2.cloned.1.call-done = bf16[1,8,4,2,128,128]{5,4,3,2,1,0:T(8,128)(2,1)} async-done(((bf16[1,8,4,2,16,128]{5,4,3,2,1,0:T(8,128)(2,1)}), bf16[1,8,4,2,128,128]{5,4,3,2,1,0:T(8,128)(2,1)}) %all-gather.2.cloned.1.call-update) | async-done | bytes 2097168 | tf_op jit(solution)/shard_map/all_gather | solution.py:86
  62.5 2.2 %gather_fusion = bf16[2,4,2,128,128]{4,3,2,1,0:T(8,128)(2,1)S(1)} fusion(bf16[8,4,2,128,128]{4,3,2,1,0:T(8,128)(2,1)} %bitcast.174, s32[1024]{0:T(1024)S(1)} %pad_clamp_fusion), kind=kCustom, calls=%fused_computation | custom fusion | bytes 1048584 | tf_op jit(solution)/shard_map/jit(_take)/gather | solution.py:87
  64.7 0.0 copy-start
  64.7 0.1 bitcast_select_fusion
  65.0 0.7 copy-done
  65.7 0.3 fusion.7
  66.0 0.3 fusion.8
  66.4 0.3 fusion.9
  66.7 0.3 fusion.10
  67.0 0.3 fusion.11
  67.3 0.3 fusion.12
  67.6 0.3 fusion.13
  68.0 0.3 fusion.14
  68.3 1.1 fusion.26
  69.3 1.1 fusion.25
  70.4 1.1 fusion.6
  71.5 1.1 fusion.5
  72.5 1.5 maximum_bitcast_fusion
  74.0 2.7 %copy.13 = f32[128,4,4,2,128,1]{4,2,1,3,5,0:T(4,128)S(1)} copy(f32[128,4,4,2,128,1]{0,4,1,2,3,5:T(8,128)} %maximum_bitcast_fusion) | data formatting | bytes 4194304 | tf_op jit(solution)/shard_map/stack | solution.py:98
  76.7 3.8 %fusion = f32[128,1,12,2,128]{4,2,3,0,1:T(8,128)} fusion(f32[128,4,4,2,128,1]{4,2,1,3,5,0:T(4,128)S(1)} %copy.13, f32[12,1,4,4,2]{0,3,2,4,1:T(4,128)S(1)} %get-tuple-element.48, f32[12,1,4,4,2]{0,3,2,4,1:T(4,128)S(1)} %get-tuple-element.47), kind=kOutput, calls=%fused_computation.7 | convolution fusion | flops 151388928 | bytes 3673088 | tf_op jit(solution)/shard_map/gostk,apstkb->apgob/dot_general | solution.py:24
  80.5 0.0 reduce-scatter.2.cloned.1.call-update
  80.6 66.7 %reduce-scatter.2.cloned.1.call-done = f32[16,1,12,2,128]{4,2,3,0,1:T(8,128)} async-done(((f32[128,1,12,2,128]{4,2,3,0,1:T(8,128)}), f32[16,1,12,2,128]{4,2,3,0,1:T(8,128)}) %reduce-scatter.2.cloned.1.call-update) | async-done | bytes 196624 | tf_op jit(solution)/shard_map/reduce_scatter | solution.py:99
  147.3 1.7 %copy.10 = f32[1,16,1,12,2,128]{5,4,3,2,1,0:T(2,128)} copy(f32[1,16,1,12,2,128]{5,3,4,1,2,0:T(8,128)} %bitcast.173) | data formatting | bytes 393216 | tf_op jit(solution)/shard_map/stack | solution.py:106
  (13 shorter events, 0.4 us)
Async XLA Ops:
  6.5 55.9 %all-gather.2.cloned.1.call-start = ((), (), s32[]{:S(2)}) async-start(), calls=%async_computation.1 | async-start | bytes 2359296 | tf_op jit(solution)/shard_map/all_gather | solution.py:86
  7.3 140.0 %reduce-scatter.2.cloned.1.call-start = ((), (), s32[]{:S(2)}) async-start(), calls=%async_computation.2 | async-start | bytes 2359296 | tf_op jit(solution)/shard_map/reduce_scatter | solution.py:99
  64.7 1.0 copy-start
Sparse Core Ops, SparseCore 0:
  9.4 53.0 all-gather.1
  80.7 66.5 reduce-scatter.1
where the time goes:
time: 156 us
  waiting for transfers between devices  117 us (75%)
  between operations  13.6 us (9%)
  matrix products  10.2 us (7%)
  local copies, waits for them, and re-layouts  9.68 us (6%)
  other arithmetic  5.64 us (4%)
    reduce_scatter x1, waiting for transfers between devices, on_device(): lax.psum_scatter(apply_gammas(jnp.stack(per_momentum, axis=1), gamma_mix,...  66.7 us
    all_gather x1, waiting for transfers between devices, on_device(): gathered = lax.all_gather(perambulator, 'space', axis=4, tiled=True)  49.2 us
    dot_general x1, matrix products, apply_gammas(): jnp.einsum('gostk,apstkb->apgob', gamma_mix, blocks, precision=lax.Precis...  3.8 us
  transfers between devices with their start and end apart: 2, of which 2 were waited for; matrix products, arithmetic and copies ran while one was open for 4% of the time, Pallas kernels for 0%

commit v1 on v0

--- a/solution.py
+++ b/solution.py
@@ -83,7 +83,7 @@
     site_ids = lax.axis_index("space") * local_sites + jnp.arange(local_sites, dtype=jnp.int32)
     cosine, sine = phase_tables(momenta, site_ids, extent_x)
     gamma_mix = gamma_mixer(gamma_columns, gamma_phases)
-    gathered = lax.all_gather(perambulator, "space", axis=4, tiled=True)
+    gathered = jnp.concatenate(lax.all_gather(perambulator, "space"), axis=4)
     chosen = jnp.take(gathered, source_slots, axis=1)
     vectors = eigvecs[0].reshape(local_sites * 3, 2 * eig_count)
     left_real, left_imag = sink_vectors(vectors, chosen[0, 0])

time: 156 us -> 156 us (level)
  no operation moved by 1% of the time
where the time goes in v1:
time: 156 us
  waiting for transfers between devices  117 us (75%)
  between operations  13.6 us (9%)
  matrix products  10.2 us (7%)
  local copies, waits for them, and re-layouts  9.68 us (6%)
  other arithmetic  5.64 us (4%)
    reduce_scatter x1, waiting for transfers between devices, on_device(): lax.psum_scatter(apply_gammas(jnp.stack(per_momentum, axis=1), gamma_mix,...  66.7 us
    all_gather x1, waiting for transfers between devices, on_device(): gathered = jnp.concatenate(lax.all_gather(perambulator, 'space'), axis=4)  49.2 us
    dot_general x1, matrix products, apply_gammas(): jnp.einsum('gostk,apstkb->apgob', gamma_mix, blocks, precision=lax.Precis...  3.8 us
  transfers between devices with their start and end apart: 2, of which 2 were waited for; matrix products, arithmetic and copies ran while one was open for 4% of the time, Pallas kernels for 0%

profile of v1, /device:TPU:0, one launch (start us, length us, event | category | flops | bytes accessed | tf_op | source)
XLA Modules:
  0.0 155.9 jit_solution(15535519684010389070)
XLA Ops:
  6.5 0.0 all-gather.3.cloned.1.call-start
  6.5 0.7 all-gather.3.cloned.1.call-update
  7.3 0.0 reduce-scatter.2.cloned.1.call-start
  7.3 1.3 fusion.137
  8.6 1.3 fusion.109
  9.9 0.1 mul.153
  10.0 0.2 mul.154
  10.2 0.1 mul.157
  10.3 0.2 mul.158
  10.5 0.7 compare_select_fusion
  11.2 0.7 convert_subtract_fusion
  11.9 0.7 fusion.124
  12.6 0.7 compare_and_fusion
  13.3 49.2 %all-gather.3.cloned.1.call-done = bf16[8,8,4,2,16,128]{5,4,0,3,2,1:T(8,128)(2,1)} async-done(((bf16[1,8,4,2,16,128]{5,4,0,3,2,1:T(8,128)(2,1)}), bf16[8,8,4,2,16,128]{5,4,0,3,2,1:T(8,128)(2,1)}) %all-gather.3.cloned.1.call-update) | async-done | bytes 2097168 | tf_op jit(solution)/shard_map/all_gather | solution.py:86
  62.5 2.2 %gather_fusion = bf16[2,4,2,128,128]{4,3,2,1,0:T(8,128)(2,1)S(1)} fusion(bf16[8,4,2,128,128]{4,3,2,1,0:T(8,128)(2,1)} %bitcast.180, s32[1024]{0:T(1024)S(1)} %pad_clamp_fusion), kind=kCustom, calls=%fused_computation | custom fusion | bytes 1048584 | tf_op jit(solution)/shard_map/jit(_take)/gather | solution.py:87
  64.7 0.0 copy-start
  64.7 0.1 bitcast_select_fusion
  65.0 0.7 copy-done
  65.7 0.3 fusion.7
  66.0 0.3 fusion.8
  66.4 0.3 fusion.9
  66.7 0.3 fusion.10
  67.0 0.3 fusion.11
  67.3 0.3 fusion.12
  67.6 0.3 fusion.13
  68.0 0.3 fusion.14
  68.3 1.1 fusion.26
  69.3 1.1 fusion.25
  70.4 1.1 fusion.6
  71.5 1.1 fusion.5
  72.5 1.5 maximum_bitcast_fusion
  74.0 2.7 %copy.14 = f32[128,4,4,2,128,1]{4,2,1,3,5,0:T(4,128)S(1)} copy(f32[128,4,4,2,128,1]{0,4,1,2,3,5:T(8,128)} %maximum_bitcast_fusion) | data formatting | bytes 4194304 | tf_op jit(solution)/shard_map/stack | solution.py:98
  76.7 3.8 %fusion = f32[128,1,12,2,128]{4,2,3,0,1:T(8,128)} fusion(f32[128,4,4,2,128,1]{4,2,1,3,5,0:T(4,128)S(1)} %copy.14, f32[12,1,4,4,2]{0,3,2,4,1:T(4,128)S(1)} %get-tuple-element.48, f32[12,1,4,4,2]{0,3,2,4,1:T(4,128)S(1)} %get-tuple-element.47), kind=kOutput, calls=%fused_computation.7 | convolution fusion | flops 151388928 | bytes 3673088 | tf_op jit(solution)/shard_map/gostk,apstkb->apgob/dot_general | solution.py:24
  80.5 0.0 reduce-scatter.2.cloned.1.call-update
  80.6 66.7 %reduce-scatter.2.cloned.1.call-done = f32[16,1,12,2,128]{4,2,3,0,1:T(8,128)} async-done(((f32[128,1,12,2,128]{4,2,3,0,1:T(8,128)}), f32[16,1,12,2,128]{4,2,3,0,1:T(8,128)}) %reduce-scatter.2.cloned.1.call-update) | async-done | bytes 196624 | tf_op jit(solution)/shard_map/reduce_scatter | solution.py:99
  147.3 1.7 %copy.11 = f32[1,16,1,12,2,128]{5,4,3,2,1,0:T(2,128)} copy(f32[1,16,1,12,2,128]{5,3,4,1,2,0:T(8,128)} %bitcast.178) | data formatting | bytes 393216 | tf_op jit(solution)/shard_map/stack | solution.py:106
  (13 shorter events, 0.4 us)
Async XLA Ops:
  6.5 55.9 %all-gather.3.cloned.1.call-start = ((), (), s32[]{:S(2)}) async-start(), calls=%async_computation.2 | async-start | bytes 2359296 | tf_op jit(solution)/shard_map/all_gather | solution.py:86
  7.3 140.0 %reduce-scatter.2.cloned.1.call-start = ((), (), s32[]{:S(2)}) async-start(), calls=%async_computation.1 | async-start | bytes 2359296 | tf_op jit(solution)/shard_map/reduce_scatter | solution.py:99
  64.7 1.0 copy-start
Sparse Core Ops, SparseCore 0:
  9.4 53.0 all-gather.2
  80.7 66.5 reduce-scatter.1
